TPU v7x, 32 devices: a whole 2x2x4 slice. The times are simulated.
32 devices in a mesh: shard: 16 (over z, y, core), model: 2 (over x).
Axes of the slice: x: 2, y: 2, z: 4, core: 2. Of those that a mesh axis runs over, the one named last changes fastest.
Arguments:
- gradients: float32 [128, 128, 4096], P(None, 'shard', 'model'), may hold values from -6 to 6
- momentum: float32 [128, 128, 4096], P(None, 'shard', 'model'), may hold values from -6 to 6
- weights: float32 [128, 128, 4096], P(None, 'shard', 'model'), may hold values from -0.1875 to 0.1875
Outputs:
- new_weights: float32 [128, 128, 4096], P(None, 'shard', 'model')
- new_momentum: float32 [128, 128, 4096], P(None, 'shard', 'model')
All inputs are finite; a program needn't handle non-finite values.
Results may differ from a plain program's by a relative error of at most 0.0001.
Values sent between devices are 32-bit elements; how exact they have to be, the bound alone decides.
A program may use at most 128 MiB of HBM per device.

v0:
```python
import jax
import jax.numpy as jnp
from jax import lax
from jax.sharding import PartitionSpec as P

ITERS = 3
hold_rate = 0.9
learn_rate = 0.9
decay_rate = 0.1


def body(gradients, momentum, weights):
    new_momentum = hold_rate * momentum + gradients
    moved = lax.all_to_all(new_momentum, "shard", split_axis=0, concat_axis=1, tiled=True)
    total = lax.psum(jnp.sum(moved * moved, axis=(1, 2), keepdims=True), "model")
    iterate = moved * lax.rsqrt(total + 1e-06)
    for step in range(ITERS):
        gram = lax.psum(
            jnp.einsum("mik,mjk->mij", iterate, iterate, precision=lax.Precision.HIGHEST), "model"
        )
        mixed = -4.775 * gram + 2.0315 * jnp.einsum(
            "mij,mjk->mik", gram, gram, precision=lax.Precision.HIGHEST
        )
        iterate = 3.4445 * iterate + jnp.einsum(
            "mij,mjk->mik", mixed, iterate, precision=lax.Precision.HIGHEST
        )
    back = lax.all_to_all(iterate, "shard", split_axis=1, concat_axis=0, tiled=True)
    new_weights = (1.0 - learn_rate * decay_rate) * weights - learn_rate * back
    return (new_weights, new_momentum)


def solution(mesh):
    placed = (P(None, "shard", "model"), P(None, "shard", "model"), P(None, "shard", "model"))
    return jax.shard_map(
        body,
        mesh=mesh,
        in_specs=placed,
        out_specs=(P(None, "shard", "model"), P(None, "shard", "model")),
        check_vma=False,
    )
```

profile of v0, /device:TPU:1, one launch (start us, length us, event | category | flops | bytes accessed | tf_op | source)
XLA Modules:
  0.0 612.2 jit_solution(11765519909520166831)
XLA Ops:
  7.2 12.0 %multiply_add_fusion.3 = f32[128,8,2048]{2,1,0:T(8,128)} fusion(f32[128,8,2048]{2,1,0:T(8,128)} %param.3, f32[128,8,2048]{2,1,0:T(8,128)} %param.4), kind=kLoop, calls=%fused_computation.7 | loop fusion | flops 4194304 | bytes 25165824 | tf_op jit(solution)/shard_map/add | solution.py:13
  19.2 189.9 %all_to_all.27 = f32[128,8,2048]{2,1,0:T(8,128)S(1)} all-to-all(f32[128,8,2048]{2,1,0:T(8,128)} %multiply_add_fusion.3), channel_id=1, replica_groups=mesh['shard'=16,'model'=2] {'shard'}, dimensions={0} | all-to-all | bytes 16777216 | tf_op jit(solution)/shard_map/all_to_all | solution.py:14
  209.1 3.4 copy-done
  212.5 0.8 fusion
  213.3 4.1 psum.28
  217.3 12.9 %fusion.2 = f32[8,128,128]{2,1,0:T(8,128)} fusion(f32[16,8,8,2048]{3,2,1,0:T(8,128)} %bitcast.38, f32[8]{0:T(128)S(1)} %rsqrt_bitcast_fusion), kind=kOutput, calls=%fused_computation.9 | convolution fusion | flops 3223322624 | bytes 8912928 | tf_op jit(solution)/shard_map/mik,mjk->mij/dot_general | solution.py:19
  230.8 28.8 %all-reduce.4.cloned.1.call-done = f32[8,128,128]{2,1,0:T(8,128)} async-done(((f32[8,128,128]{2,1,0:T(8,128)}), f32[8,128,128]{2,1,0:T(8,128)}) %all-reduce.4.cloned.1.call-update) | async-done | bytes 524304 | tf_op jit(solution)/shard_map/psum | solution.py:18
  259.6 2.1 fusion.7
  261.7 11.7 %multiply_add_fusion.2 = f32[8,128,2048]{2,1,0:T(8,128)S(1)} fusion(f32[16,8,8,2048]{3,2,1,0:T(8,128)} %bitcast.39, f32[8,128,128]{2,1,0:T(8,128)S(1)} %fusion.7, f32[8]{0:T(128)S(1)} %rsqrt_bitcast_fusion), kind=kOutput, calls=%fused_computation.6 | convolution fusion | flops 3229614080 | bytes 17301536 | tf_op jit(solution)/shard_map/mij,mjk->mik/dot_general | solution.py:24
  273.4 3.4 copy-done.1
  276.8 8.5 %fusion.8 = f32[8,128,128]{2,1,0:T(8,128)} fusion(f32[8,128,2048]{2,1,0:T(8,128)S(1)} %multiply_add_fusion.2), kind=kOutput, calls=%fused_computation.20 | convolution fusion | flops 3221225472 | bytes 8912896 | tf_op jit(solution)/shard_map/mik,mjk->mij/dot_general | solution.py:19
  285.4 28.8 %all-reduce.6.cloned.1.call-done = f32[8,128,128]{2,1,0:T(8,128)} async-done(((f32[8,128,128]{2,1,0:T(8,128)}), f32[8,128,128]{2,1,0:T(8,128)}) %all-reduce.6.cloned.1.call-update) | async-done | bytes 524304 | tf_op jit(solution)/shard_map/psum | solution.py:18
  314.1 2.1 fusion.6
  316.2 14.1 %multiply_add_fusion.1 = f32[8,128,2048]{2,1,0:T(8,128)S(1)} fusion(f32[8,128,2048]{2,1,0:T(8,128)} %copy-done.1, f32[8,128,128]{2,1,0:T(8,128)S(1)} %fusion.6), kind=kOutput, calls=%fused_computation.5 | convolution fusion | flops 3225419776 | bytes 17301504 | tf_op jit(solution)/shard_map/mij,mjk->mik/dot_general | solution.py:24
  330.3 3.4 copy-done.2
  333.7 8.5 %fusion.9 = f32[8,128,128]{2,1,0:T(8,128)} fusion(f32[8,128,2048]{2,1,0:T(8,128)S(1)} %multiply_add_fusion.1), kind=kOutput, calls=%fused_computation.21 | convolution fusion | flops 3221225472 | bytes 8912896 | tf_op jit(solution)/shard_map/mik,mjk->mij/dot_general | solution.py:19
  342.3 28.8 %all-reduce.8.cloned.1.call-done = f32[8,128,128]{2,1,0:T(8,128)} async-done(((f32[8,128,128]{2,1,0:T(8,128)}), f32[8,128,128]{2,1,0:T(8,128)}) %all-reduce.8.cloned.1.call-update) | async-done | bytes 524304 | tf_op jit(solution)/shard_map/psum | solution.py:18
  371.1 2.1 fusion.5
  373.2 15.0 %multiply_add_fusion = f32[8,128,2048]{2,1,0:T(8,128)S(1)} fusion(f32[8,128,2048]{2,1,0:T(8,128)} %copy-done.2, f32[8,128,128]{2,1,0:T(8,128)S(1)} %fusion.5), kind=kOutput, calls=%fused_computation.4 | convolution fusion | flops 3225419776 | bytes 17301504 | tf_op jit(solution)/shard_map/mij,mjk->mik/dot_general | solution.py:24
  388.2 4.9 copy.8
  393.1 188.9 %all_to_all.28 = f32[8,128,2048]{2,0,1:T(8,128)S(1)} all-to-all(f32[8,128,2048]{2,0,1:T(8,128)S(1)} %copy.8), channel_id=1, replica_groups=mesh['shard'=16,'model'=2] {'shard'}, dimensions={1} | all-to-all | bytes 16777216 | tf_op jit(solution)/shard_map/all_to_all | solution.py:27
  581.9 1.8 broadcast_multiply_fusion
  583.8 9.7 %copy.9 = f32[16,8,8,2048]{3,2,1,0:T(8,128)} copy(f32[16,8,8,2048]{3,1,2,0:T(8,128)S(1)} %bitcast.40) | data formatting | bytes 16777216 | tf_op jit(solution)/shard_map/mul | solution.py:28
  593.5 12.0 %bitcast_subtract_fusion = f32[128,8,2048]{2,1,0:T(8,128)} fusion(f32[16,8,8,2048]{3,2,1,0:T(8,128)} %copy.9, f32[128,8,2048]{2,1,0:T(8,128)} %param.5), kind=kLoop, calls=%fused_computation.1 | loop fusion | flops 4194304 | bytes 25165824 | tf_op jit(solution)/shard_map/sub | solution.py:28
  (10 shorter events, 0.7 us)
Async XLA Ops:
  7.2 252.5 %all-reduce.4.cloned.1.call-start = ((), (), s32[]{:S(2)}) async-start(), calls=%async_computation.2 | async-start | bytes 1048576 | tf_op jit(solution)/shard_map/psum | solution.py:18
  209.1 3.4 copy-start
  230.3 83.9 %all-reduce.6.cloned.1.call-start = ((), (), s32[]{:S(2)}) async-start(), calls=%async_computation.3 | async-start | bytes 1048576 | tf_op jit(solution)/shard_map/psum | solution.py:18
  273.4 3.4 copy-start.1
  285.3 85.8 %all-reduce.8.cloned.1.call-start = ((), (), s32[]{:S(2)}) async-start(), calls=%async_computation.4 | async-start | bytes 1048576 | tf_op jit(solution)/shard_map/psum | solution.py:18
  330.3 3.4 copy-start.2
Sparse Core Ops, SparseCore 0:
  230.4 29.1 all-reduce.3
  285.4 28.6 all-reduce.5
  342.4 28.6 all-reduce.7
where the time goes:
time: 618 us; the launch traced here: 612 us
  blocking collectives  383 us (62%)
  waiting for transfers between devices  86.4 us (14%)
  matrix products  76.9 us (12%)
  other arithmetic  26.6 us (4%)
  local copies, waits for them, and re-layouts  24.7 us (4%)
  between operations  14 us (2%)
    all_to_all x1, blocking collectives, body(): lax.all_to_all(new_momentum, 'shard', split_axis=0, concat_axis=1, tiled=...  190 us
    all_to_all x1, blocking collectives, body(): lax.all_to_all(iterate, 'shard', split_axis=1, concat_axis=0, tiled=True)  189 us
    psum x3, waiting for transfers between devices, body(): lax.psum(jnp.einsum('mik,mjk->mij', iterate, iterate, precision=lax.Preci...  86.4 us
    dot_general x3, matrix products, body(): jnp.einsum('mij,mjk->mik', mixed, iterate, precision=lax.Precision.HIGHEST)  40.8 us
    dot_general x3, matrix products, body(): jnp.einsum('mik,mjk->mij', iterate, iterate, precision=lax.Precision.HIGH...  29.9 us
  transfers between devices with their start and end apart: 3, of which 3 were waited for; matrix products, arithmetic and copies ran while one was open for 0% of the time, Pallas kernels for 0%

commit v1 on v0

--- a/solution.py
+++ b/solution.py
@@ -15,8 +15,12 @@
     total = lax.psum(jnp.sum(moved * moved, axis=(1, 2), keepdims=True), "model")
     iterate = moved * lax.rsqrt(total + 1e-06)
     for step in range(ITERS):
-        gram = lax.psum(
-            jnp.einsum("mik,mjk->mij", iterate, iterate, precision=lax.Precision.HIGHEST), "model"
+        gram = jnp.sum(
+            lax.all_gather(
+                jnp.einsum("mik,mjk->mij", iterate, iterate, precision=lax.Precision.HIGHEST),
+                "model",
+            ),
+            axis=0,
         )
         mixed = -4.775 * gram + 2.0315 * jnp.einsum(
             "mij,mjk->mik", gram, gram, precision=lax.Precision.HIGHEST

time: 618 us -> 596 us (0.964)
  waiting for transfers between devices: 86.4 us -> 64.3 us
    psum x3 -> x0, waiting for transfers between devices: 86.4 us -> none  [body(): lax.psum(jnp.einsum('mik,mjk->mij', iterate, iterate, precision=lax.Preci...]
    all_gather x0 -> x3, waiting for transfers between devices: none -> 64.2 us  [body(): lax.all_gather(jnp.einsum('mik,mjk->mij', iterate, iterate, precision=lax...]
where the time goes in v1:
time: 596 us; the launch traced here: 590 us
  blocking collectives  383 us (64%)
  matrix products  72.7 us (12%)
  waiting for transfers between devices  64.3 us (11%)
  other arithmetic  30.6 us (5%)
  local copies, waits for them, and re-layouts  24.7 us (4%)
  between operations  14 us (2%)
    all_to_all x1, blocking collectives, body(): lax.all_to_all(new_momentum, 'shard', split_axis=0, concat_axis=1, tiled=...  190 us
    all_to_all x1, blocking collectives, body(): lax.all_to_all(iterate, 'shard', split_axis=1, concat_axis=0, tiled=True)  189 us
    all_gather x3, waiting for transfers between devices, body(): lax.all_gather(jnp.einsum('mik,mjk->mij', iterate, iterate, precision=lax...  64.2 us
    dot_general x3, matrix products, body(): jnp.einsum('mij,mjk->mik', mixed, iterate, precision=lax.Precision.HIGHEST)  40.8 us
    dot_general x3, matrix products, body(): jnp.einsum('mik,mjk->mij', iterate, iterate, precision=lax.Precision.HIGH...  30 us
    add x1, other arithmetic, body(): new_momentum = hold_rate * momentum + gradients  12 us
    sub x1, other arithmetic, body(): new_weights = (1.0 - learn_rate * decay_rate) * weights - learn_rate * back  12 us
  transfers between devices with their start and end apart: 3, of which 3 were waited for; matrix products, arithmetic and copies ran while one was open for 0% of the time, Pallas kernels for 0%

profile of v1, /device:TPU:1, one launch (start us, length us, event | category | flops | bytes accessed | tf_op | source)
XLA Modules:
  0.0 589.9 jit_solution(12277200981906233546)
XLA Ops:
  7.2 12.0 %multiply_add_fusion.3 = f32[128,8,2048]{2,1,0:T(8,128)} fusion(f32[128,8,2048]{2,1,0:T(8,128)} %param.3, f32[128,8,2048]{2,1,0:T(8,128)} %param.4), kind=kLoop, calls=%fused_computation.7 | loop fusion | flops 4194304 | bytes 25165824 | tf_op jit(solution)/shard_map/add | solution.py:13
  19.2 189.9 %all_to_all.27 = f32[128,8,2048]{2,1,0:T(8,128)S(1)} all-to-all(f32[128,8,2048]{2,1,0:T(8,128)} %multiply_add_fusion.3), channel_id=1, replica_groups=mesh['shard'=16,'model'=2] {'shard'}, dimensions={0} | all-to-all | bytes 16777216 | tf_op jit(solution)/shard_map/all_to_all | solution.py:14
  209.1 3.4 copy-done
  212.5 0.8 fusion
  213.3 4.1 psum.7
  217.3 12.9 %fusion.2 = f32[8,128,128]{2,1,0:T(8,128)} fusion(f32[16,8,8,2048]{3,2,1,0:T(8,128)} %bitcast.41, f32[8]{0:T(128)S(1)} %rsqrt_bitcast_fusion), kind=kOutput, calls=%fused_computation.9 | convolution fusion | flops 3223322624 | bytes 8912928 | tf_op jit(solution)/shard_map/mik,mjk->mij/dot_general | solution.py:20
  230.8 21.4 %all-gather.7.cloned.1.call-done = f32[16,128,128]{2,1,0:T(8,128)} async-done(((f32[8,128,128]{2,1,0:T(8,128)}), f32[16,128,128]{2,1,0:T(8,128)}) %all-gather.7.cloned.1.call-update) | async-done | bytes 1048592 | tf_op jit(solution)/shard_map/all_gather | solution.py:19
  252.3 1.3 reduce_sum.37
  254.3 11.7 %multiply_add_fusion.2 = f32[8,128,2048]{2,1,0:T(8,128)S(1)} fusion(f32[16,8,8,2048]{3,2,1,0:T(8,128)} %bitcast.42, f32[8,128,128]{2,1,0:T(8,128)S(1)} %fusion.7, f32[8]{0:T(128)S(1)} %rsqrt_bitcast_fusion), kind=kOutput, calls=%fused_computation.6 | convolution fusion | flops 3229614080 | bytes 17301536 | tf_op jit(solution)/shard_map/mij,mjk->mik/dot_general | solution.py:28
  266.0 3.4 copy-done.1
  269.3 8.5 %fusion.8 = f32[8,128,128]{2,1,0:T(8,128)} fusion(f32[8,128,2048]{2,1,0:T(8,128)S(1)} %multiply_add_fusion.2), kind=kOutput, calls=%fused_computation.20 | convolution fusion | flops 3221225472 | bytes 8912896 | tf_op jit(solution)/shard_map/mik,mjk->mij/dot_general | solution.py:20
  278.0 21.4 %all-gather.9.cloned.1.call-done = f32[16,128,128]{2,1,0:T(8,128)} async-done(((f32[8,128,128]{2,1,0:T(8,128)}), f32[16,128,128]{2,1,0:T(8,128)}) %all-gather.9.cloned.1.call-update) | async-done | bytes 1048592 | tf_op jit(solution)/shard_map/all_gather | solution.py:19
  299.3 1.3 reduce_sum.38
  301.3 14.1 %multiply_add_fusion.1 = f32[8,128,2048]{2,1,0:T(8,128)S(1)} fusion(f32[8,128,2048]{2,1,0:T(8,128)} %copy-done.1, f32[8,128,128]{2,1,0:T(8,128)S(1)} %fusion.6), kind=kOutput, calls=%fused_computation.5 | convolution fusion | flops 3225419776 | bytes 17301504 | tf_op jit(solution)/shard_map/mij,mjk->mik/dot_general | solution.py:28
  315.5 3.4 copy-done.2
  318.9 8.5 %fusion.9 = f32[8,128,128]{2,1,0:T(8,128)} fusion(f32[8,128,2048]{2,1,0:T(8,128)S(1)} %multiply_add_fusion.1), kind=kOutput, calls=%fused_computation.21 | convolution fusion | flops 3221225472 | bytes 8912896 | tf_op jit(solution)/shard_map/mik,mjk->mij/dot_general | solution.py:20
  327.4 21.4 %all-gather.11.cloned.1.call-done = f32[16,128,128]{2,1,0:T(8,128)} async-done(((f32[8,128,128]{2,1,0:T(8,128)}), f32[16,128,128]{2,1,0:T(8,128)}) %all-gather.11.cloned.1.call-update) | async-done | bytes 1048592 | tf_op jit(solution)/shard_map/all_gather | solution.py:19
  348.9 1.3 reduce_sum.39
  350.9 15.0 %multiply_add_fusion = f32[8,128,2048]{2,1,0:T(8,128)S(1)} fusion(f32[8,128,2048]{2,1,0:T(8,128)} %copy-done.2, f32[8,128,128]{2,1,0:T(8,128)S(1)} %fusion.5), kind=kOutput, calls=%fused_computation.4 | convolution fusion | flops 3225419776 | bytes 17301504 | tf_op jit(solution)/shard_map/mij,mjk->mik/dot_general | solution.py:28
  365.9 4.9 copy.8
  370.8 188.9 %all_to_all.28 = f32[8,128,2048]{2,0,1:T(8,128)S(1)} all-to-all(f32[8,128,2048]{2,0,1:T(8,128)S(1)} %copy.8), channel_id=1, replica_groups=mesh['shard'=16,'model'=2] {'shard'}, dimensions={1} | all-to-all | bytes 16777216 | tf_op jit(solution)/shard_map/all_to_all | solution.py:31
  559.6 1.8 broadcast_multiply_fusion
  561.5 9.7 %copy.9 = f32[16,8,8,2048]{3,2,1,0:T(8,128)} copy(f32[16,8,8,2048]{3,1,2,0:T(8,128)S(1)} %bitcast.43) | data formatting | bytes 16777216 | tf_op jit(solution)/shard_map/mul | solution.py:32
  571.2 12.0 %bitcast_subtract_fusion = f32[128,8,2048]{2,1,0:T(8,128)} fusion(f32[16,8,8,2048]{3,2,1,0:T(8,128)} %copy.9, f32[128,8,2048]{2,1,0:T(8,128)} %param.5), kind=kLoop, calls=%fused_computation.1 | loop fusion | flops 4194304 | bytes 25165824 | tf_op jit(solution)/shard_map/sub | solution.py:32
  (13 shorter events, 2.7 us)
Async XLA Ops:
  7.2 245.1 %all-gather.7.cloned.1.call-start = ((), (), s32[]{:S(2)}) async-start(), calls=%async_computation.2 | async-start | bytes 1572864 | tf_op jit(solution)/shard_map/all_gather | solution.py:19
  209.1 3.4 copy-start
  230.3 69.1 %all-gather.9.cloned.1.call-start = ((), (), s32[]{:S(2)}) async-start(), calls=%async_computation.3 | async-start | bytes 1572864 | tf_op jit(solution)/shard_map/all_gather | solution.py:19
  265.9 3.4 copy-start.1
  277.9 71.0 %all-gather.11.cloned.1.call-start = ((), (), s32[]{:S(2)}) async-start(), calls=%async_computation.4 | async-start | bytes 1572864 | tf_op jit(solution)/shard_map/all_gather | solution.py:19
  315.5 3.4 copy-start.2
Sparse Core Ops, SparseCore 0:
  230.4 21.8 all-gather.6
  278.0 21.2 all-gather.8
  327.5 21.2 all-gather.10
